TPU v7x, 256 devices: a whole 4x4x8 slice. The times are simulated.
256 devices in a mesh: sa: 32 (over z_lo, x, core), sb: 8 (over z_hi, y).
Axes of the slice: x: 4, y: 4, z: 8 (z_hi: 2, z_lo: 4; z = z_hi * 4 + z_lo), core: 2. Of those that a mesh axis runs over, the one named last changes fastest.
Arguments:
- tokens: bfloat16 [64, 32, 32, 2048], P('sa', 'sb'), may hold values from -6 to 6
- norm_gain: float32 [2048], replicated, may hold values from 0.5 to 1.5
- gate_weight: bfloat16 [2048, 2048], P(('sa', 'sb')), may hold values from -0.125 to 0.125
- level_one: bfloat16 [32, 32, 64, 64], P('sb', 'sa'), may hold values from -0.75 to 0.75
- level_two: bfloat16 [64, 32, 32, 32], P('sa', 'sb'), may hold values from -1 to 1
- level_three: bfloat16 [64, 32, 32, 32], P('sa', 'sb'), may hold values from -1 to 1
- upstream: bfloat16 [64, 32, 32, 2048], P('sa', 'sb'), may hold values from -6 to 6
Outputs:
- output: bfloat16 [64, 32, 32, 2048], P('sa', 'sb')
- grad_tokens: bfloat16 [64, 32, 32, 2048], P('sa', 'sb')
- grad_one: float32 [32, 32, 64, 64], P('sb', 'sa')
- grad_two: float32 [64, 32, 32, 32], P('sa', 'sb')
- grad_three: float32 [64, 32, 32, 32], P('sa', 'sb')
All inputs are finite; a program needn't handle non-finite values.
Results may differ from a plain program's by a relative error of at most 0.0071.
Values may be sent and summed in bfloat16 or wider, within the bound.
A program may use at most 128 MiB of HBM per device.

v0:
```python
import jax
import jax.numpy as jnp
from jax import lax
from jax.sharding import PartitionSpec as P

ALL = ("sa", "sb")
EPSILON = 1e-06


def to_blocks(values):
    i, j, k, c = values.shape
    sa, sb = (lax.axis_size("sa"), lax.axis_size("sb"))
    parts = values.reshape(i, j, sa, sb, c // sb).transpose(2, 3, 0, 1, 4)
    parts = parts.reshape(sa * sb, i * j, c // sb)
    parts = lax.all_to_all(parts, ALL, split_axis=0, concat_axis=0, tiled=True)
    parts = parts.reshape(sa, sb, i, j, c // sb).transpose(0, 2, 1, 3, 4)
    return parts.reshape(sa * i, sb * j, c // sb)


def from_blocks(values):
    sa, sb = (lax.axis_size("sa"), lax.axis_size("sb"))
    i, j, c = (values.shape[0] // sa, values.shape[1] // sb, values.shape[2])
    parts = values.reshape(sa, i, sb, j, c).transpose(0, 2, 1, 3, 4)
    parts = parts.reshape(sa * sb, i * j, c)
    parts = lax.all_to_all(parts, ALL, split_axis=0, concat_axis=0, tiled=True)
    parts = parts.reshape(sa, sb, i, j, c).transpose(2, 3, 0, 1, 4)
    return parts.reshape(i, j, sa, sb * c)


def dot(pattern, left, right):
    return jnp.einsum(pattern, left, right, preferred_element_type=jnp.float32)


def body(tokens, norm_gain, gate_weight, level_one, level_two, level_three, upstream):
    channels = tokens.shape[3]
    sa, sb = (lax.axis_size("sa"), lax.axis_size("sb"))
    grad_scale = channels ** (-0.5)
    gathered = lax.all_gather(gate_weight, ALL, axis=0, tiled=True)
    block_one = lax.all_gather(level_one[:, 0], "sb", axis=0, tiled=True)
    block_two = lax.all_gather(level_two, "sb", axis=1, tiled=True)
    block_two = lax.all_to_all(block_two, "sa", split_axis=1, concat_axis=0, tiled=True)[:, 0]
    tokens_float = tokens.astype(jnp.float32)
    inverse_rms = lax.rsqrt(jnp.mean(tokens_float * tokens_float, axis=3, keepdims=True) + EPSILON)
    normed = (tokens_float * inverse_rms * norm_gain).astype(jnp.bfloat16)
    normed_block = to_blocks(normed)
    first_mix = dot("joi,ijc->ojc", block_one, normed_block).astype(jnp.bfloat16)
    second_mix = dot("ioj,ijc->ioc", block_two, first_mix).astype(jnp.bfloat16)
    second_mix = from_blocks(second_mix)
    mixed_all = dot("ijok,ijkc->ijoc", level_three, second_mix)
    token_rows = normed.reshape(-1, channels)
    gate_pre = dot("tr,rc->tc", token_rows, gathered).reshape(tokens.shape)
    gate_sigmoid = jax.nn.sigmoid(gate_pre)
    gate_value = gate_pre * gate_sigmoid
    output = (tokens_float + mixed_all * gate_value).astype(jnp.bfloat16)
    upstream_float = upstream.astype(jnp.float32)
    grad_mixed = (upstream_float * gate_value).astype(jnp.bfloat16)
    grad_gate = (
        upstream_float * mixed_all * gate_sigmoid * (1.0 + gate_pre * (1.0 - gate_sigmoid))
    ).astype(jnp.bfloat16)
    grad_second = dot("ijok,ijoc->ijkc", level_three, grad_mixed).astype(jnp.bfloat16)
    grad_block = to_blocks(grad_second)
    grad_first = dot("ioj,ioc->ijc", block_two, grad_block).astype(jnp.bfloat16)
    grad_normed = dot("joi,ojc->ijc", block_one, grad_first).astype(jnp.bfloat16)
    grad_normed = from_blocks(grad_normed)
    grad_three = dot("ijoc,ijkc->ijok", grad_mixed, second_mix) * grad_scale
    part_two = dot("ioc,ijc->ioj", grad_block, first_mix).astype(jnp.bfloat16)
    part_one = dot("ojc,ijc->joi", grad_first, normed_block).astype(jnp.bfloat16)
    part_two = lax.all_to_all(part_two[:, None], "sa", split_axis=0, concat_axis=1, tiled=True)
    m1, m2 = (part_one.shape[1], part_two.shape[2])
    own_i, own_k = (part_two.shape[0], part_two.shape[1] // sb)
    own_j = part_one.shape[0] // sb
    packed = jnp.concatenate(
        [
            part_one.reshape(sb, -1),
            part_two.reshape(own_i, sb, own_k, m2, m2).transpose(1, 0, 2, 3, 4).reshape(sb, -1),
        ],
        axis=1,
    )
    packed = lax.all_to_all(packed, "sb", split_axis=0, concat_axis=0, tiled=True)
    summed = jnp.sum(packed.astype(jnp.float32), axis=0) * grad_scale
    cut = own_j * m1 * m1
    grad_one = summed[:cut].reshape(own_j, 1, m1, m1)
    grad_two = summed[cut:].reshape(own_i, own_k, m2, m2)
    back_term = dot("tc,rc->tr", grad_gate.reshape(-1, channels), gathered)
    grad_hidden = grad_normed.astype(jnp.float32) + back_term.reshape(tokens.shape)
    weighted = grad_hidden * norm_gain
    average = jnp.mean(weighted * tokens_float, axis=3, keepdims=True)
    grad_tokens = (
        upstream_float + inverse_rms * weighted - tokens_float * inverse_rms**3 * average
    ).astype(jnp.bfloat16)
    return (output, grad_tokens, grad_one, grad_two, grad_three)


def solution(mesh):
    token_spec = P("sa", "sb", None, None)
    block_spec = P("sb", "sa", None, None)
    in_specs = (token_spec, P(), P(ALL, None), block_spec, token_spec, token_spec, token_spec)
    out_specs = (token_spec, token_spec, block_spec, token_spec, token_spec)
    return jax.shard_map(body, mesh=mesh, in_specs=in_specs, out_specs=out_specs, check_vma=False)
```

profile of v0, /device:TPU:1, one launch (start us, length us, event | category | flops | bytes accessed | tf_op | source)
XLA Modules:
  0.0 908.0 jit_solution(1630995716396295364)
XLA Ops:
  7.2 0.7 all-gather.3.cloned.1.call-update
  7.9 0.8 copy.129
  8.8 42.1 %all_gather.10 = bf16[2,32,32,32]{3,2,0,1:T(8,128)(2,1)S(1)} all-gather(bf16[2,4,32,32]{3,2,0,1:T(8,128)(2,1)S(1)} %copy.129), channel_id=1, replica_groups=mesh['sa'=32,'sb'=8] {'sb'}, dimensions={1}, use_global_device_ids=true | all-gather | bytes 147456 | tf_op jit(solution)/shard_map/all_gather | solution.py:40
  50.8 1.2 reshape.141
  52.0 12.8 %all-to-all-start.1 = ((bf16[32,2,1024]{2,1,0:T(2,128)(2,1)}), bf16[32,2,1024]{2,1,0:T(2,128)(2,1)S(1)}, u32[]{:S(2)}, u32[]{:S(2)}) async-start(bf16[32,2,1024]{2,1,0:T(2,128)(2,1)} %reshape.141), calls=%async_computation.1 | async-start | bytes 262144 | tf_op jit(solution)/shard_map/all_to_all | solution.py:41
  64.8 0.3 fusion.16
  65.1 0.3 fusion.18
  65.4 0.3 copy.159
  65.7 1.6 copy.154
  67.3 6.0 all-to-all-done.1
  73.3 9.9 %all-to-all-start = ((bf16[256,8,256]{2,1,0:T(8,128)(2,1)}), bf16[256,8,256]{2,1,0:T(8,128)(2,1)S(1)}, u32[]{:S(2)}, u32[]{:S(2)}) async-start(bf16[256,8,256]{2,1,0:T(8,128)(2,1)} %copy.154), calls=%async_computation | async-start | bytes 2097152 | tf_op jit(solution)/shard_map/all_to_all | solution.py:15
  83.2 60.6 %all-gather = bf16[32,1,64,64]{3,2,1,0:T(8,128)(2,1)S(1)} all-gather(bf16[4,1,64,64]{3,2,1,0:T(8,128)(2,1)S(1)} %copy-done.11), channel_id=2, replica_groups=mesh['sa'=32,'sb'=8] {'sb'}, dimensions={0}, use_global_device_ids=true | all-gather | bytes 294912 | tf_op jit(solution)/shard_map/all_gather | solution.py:39
  143.8 0.3 reshape.142
  144.1 0.2 copy.127
  144.3 1.1 copy.128
  145.4 0.4 reshape.123
  145.8 0.4 fusion.25
  146.3 1.7 fusion.26
  148.0 1.3 reshape.124
  149.5 0.6 copy.132
  150.1 42.8 %all_to_all.59 = bf16[256,8,256]{2,1,0:T(8,128)(2,1)S(1)} all-to-all(bf16[256,8,256]{2,1,0:T(8,128)(2,1)S(1)} %copy.132), channel_id=1, replica_groups=mesh['sa'=32,'sb'=8] {'sa','sb'}, dimensions={0} | all-to-all | bytes 2097152 | tf_op jit(solution)/shard_map/all_to_all | solution.py:25
  192.8 1.2 copy.155
  194.0 1.6 reshape.127
  195.6 1.8 convolution_bitcast_fusion
  197.4 546.0 %all-gather.3.cloned.1.call-done = bf16[2048,2048]{1,0:T(8,128)(2,1)} async-done(((bf16[8,2048]{1,0:T(8,128)(2,1)}), bf16[2048,2048]{1,0:T(8,128)(2,1)}) %all-gather.3.cloned.1.call-update) | async-done | bytes 8388624 | tf_op jit(solution)/shard_map/all_gather | solution.py:38
  743.4 9.3 %fusion.10 = (bf16[2,4,32,2048]{3,2,1,0:T(8,128)(2,1)S(1)}, bf16[2,4,32,2048]{3,2,1,0:T(8,128)(2,1)}, f32[2,4,32,2048]{3,2,1,0:T(8,128)}) fusion(bf16[2,4,32,2048]{3,2,1,0:T(8,128)(2,1)} %param.13, f32[2,4,32,2048]{3,2,1,0:T(8,128)} %convolution_bitcast_fusion, bf16[2,4,32,2048]{3,2,1,0:T(8,128)(2,1)} %param.7, ...), kind=kOutput, calls=%fused_computation.16 | convolution fusion | flops 2155347968 | bytes 16786432 | tf_op jit(solution)/shard_map/tr,rc->tc/dot_general | solution.py:31
  752.7 0.5 convolution_convert_fusion
  753.2 0.3 copy.160
  753.5 0.2 copy-done.8
  753.8 0.6 copy.156
  754.4 44.5 %all_to_all.60 = bf16[256,8,256]{2,1,0:T(8,128)(2,1)S(1)} all-to-all(bf16[256,8,256]{2,1,0:T(8,128)(2,1)S(1)} %copy.156), channel_id=1, replica_groups=mesh['sa'=32,'sb'=8] {'sa','sb'}, dimensions={0} | all-to-all | bytes 2097152 | tf_op jit(solution)/shard_map/all_to_all | solution.py:15
  798.9 0.2 copy.136
  799.1 2.3 copy.137
  801.4 2.1 reshape.131
  803.5 2.9 fusion.27
  806.4 0.5 fusion.23
  806.9 2.2 reshape.143
  809.2 5.9 all-to-all-start.5
  815.0 1.5 convolution_convert_fusion.6
  816.6 1.5 reshape.134
  818.1 5.6 all-to-all-done.5
  823.7 1.2 reshape.144
  825.0 1.2 reshape.136
  826.2 0.9 maximum_bitcast_fusion
  827.2 0.5 broadcast.59
  827.7 1.6 reduce.1
  829.3 2.0 reshape.145
  831.3 4.1 all-to-all-start.6
  835.4 1.9 fusion.24
  837.3 1.5 reshape.132
  838.8 0.6 copy.141
  839.4 1.6 copy.142
  841.0 6.0 all-to-all-done.6
  846.9 10.8 %all-to-all-start.4 = ((bf16[256,8,256]{2,1,0:T(8,128)(2,1)}), bf16[256,8,256]{2,1,0:T(8,128)(2,1)}, u32[]{:S(2)}, u32[]{:S(2)}) async-start(bf16[256,8,256]{2,1,0:T(8,128)(2,1)} %copy.142), calls=%async_computation.4 | async-start | bytes 2097152 | tf_op jit(solution)/shard_map/all_to_all | solution.py:25
  857.8 1.1 convolution_multiply_fusion
  858.8 2.6 reshape.146
  861.4 1.0 convert_reduce_fusion
  862.5 0.7 slice.15
  863.2 0.7 slice.17
  863.9 24.2 %all-to-all-done.4 = bf16[256,8,256]{2,1,0:T(8,128)(2,1)} async-done(((bf16[256,8,256]{2,1,0:T(8,128)(2,1)}), bf16[256,8,256]{2,1,0:T(8,128)(2,1)}, u32[]{:S(2)}, u32[]{:S(2)}) %all-to-all-start.4) | async-done | bytes 1048608 | tf_op jit(solution)/shard_map/all_to_all | solution.py:25
  888.1 1.4 copy.157
  889.6 1.5 reshape.137
  891.1 8.4 fusion.21
  899.6 1.6 fusion.15
  (34 shorter events, 0.3 us)
Async XLA Ops:
  7.2 188.4 %copy-start = (bf16[2,4,32,32]{3,2,1,0:T(8,128)(2,1)S(1)}, bf16[2,4,32,32]{3,2,1,0:T(8,128)(2,1)}, u32[]{:S(2)}) copy-start(bf16[2,4,32,32]{3,2,1,0:T(8,128)(2,1)} %param.12) | copy-start | bytes 49156
  7.2 57.6 %copy-start.2 = (bf16[2,4,32,2048]{3,2,1,0:T(8,128)(2,1)S(1)}, bf16[2,4,32,2048]{3,2,1,0:T(8,128)(2,1)}, u32[]{:S(2)}) copy-start(bf16[2,4,32,2048]{3,2,1,0:T(8,128)(2,1)} %param.7) | copy-start | bytes 3145732
  7.2 57.9 %copy-start.12 = (f32[2048]{0:T(1024)S(1)}, f32[2048]{0:T(1024)}, u32[]{:S(2)}) copy-start(f32[2048]{0:T(1024)} %param.8) | copy-start | bytes 24580
  7.2 736.2 %all-gather.3.cloned.1.call-start = ((), (), s32[]{:S(2)}) async-start(), calls=%async_computation.7 | async-start | bytes 8421376 | tf_op jit(solution)/shard_map/all_gather | solution.py:38
  52.0 21.3 %all-to-all-start.1 = ((bf16[32,2,1024]{2,1,0:T(2,128)(2,1)}), bf16[32,2,1024]{2,1,0:T(2,128)(2,1)S(1)}, u32[]{:S(2)}, u32[]{:S(2)}) async-start(bf16[32,2,1024]{2,1,0:T(2,128)(2,1)} %reshape.141), calls=%async_computation.1 | async-start | bytes 262144 | tf_op jit(solution)/shard_map/all_to_all | solution.py:41
  65.7 17.5 %copy-start.11 = (bf16[4,1,64,64]{3,2,1,0:T(8,128)(2,1)S(1)}, bf16[4,1,64,64]{3,2,1,0:T(8,128)(2,1)}, u32[]{:S(2)}) copy-start(bf16[4,1,64,64]{3,2,1,0:T(8,128)(2,1)} %param.10) | copy-start | bytes 98308
  73.3 70.8 %all-to-all-start = ((bf16[256,8,256]{2,1,0:T(8,128)(2,1)}), bf16[256,8,256]{2,1,0:T(8,128)(2,1)S(1)}, u32[]{:S(2)}, u32[]{:S(2)}) async-start(bf16[256,8,256]{2,1,0:T(8,128)(2,1)} %copy.154), calls=%async_computation | async-start | bytes 2097152 | tf_op jit(solution)/shard_map/all_to_all | solution.py:15
  143.8 2.0 copy-start.6
  144.1 2.2 copy-start.4
  752.7 1.0 copy-start.8
  803.5 2.9 copy-start.1
  803.5 2.9 copy-start.5
  809.2 14.6 %all-to-all-start.5 = ((bf16[32,2,1024]{2,1,0:T(2,128)(2,1)}), bf16[32,2,1024]{2,1,0:T(2,128)(2,1)}, u32[]{:S(2)}, u32[]{:S(2)}) async-start(bf16[32,2,1024]{2,1,0:T(2,128)(2,1)} %reshape.143), calls=%async_computation.5 | async-start | bytes 262144 | tf_op jit(solution)/shard_map/all_to_all | solution.py:68
  825.0 10.4 %copy-start.7 = (bf16[32,1,64,64]{3,2,1,0:T(8,128)(2,1)S(1)}, bf16[32,1,64,64]{3,2,1,0:T(8,128)(2,1)}, u32[]{:S(2)}) copy-start(bf16[32,1,64,64]{3,2,1,0:T(8,128)(2,1)} %copy-done.6) | copy-start | bytes 786436
  831.3 15.6 %all-to-all-start.6 = ((bf16[8,2,12288]{2,1,0:T(2,128)(2,1)}), bf16[8,2,12288]{2,1,0:T(2,128)(2,1)}, u32[]{:S(2)}, u32[]{:S(2)}) async-start(bf16[8,2,12288]{2,1,0:T(2,128)(2,1)} %reshape.145), calls=%async_computation.6 | async-start | bytes 786432 | tf_op jit(solution)/shard_map/all_to_all | solution.py:79
  839.4 18.3 %copy-start.9 = (bf16[2,4,32,2048]{3,2,1,0:T(8,128)(2,1)S(1)}, bf16[2,4,32,2048]{3,2,1,0:T(8,128)(2,1)}, u32[]{:S(2)}) copy-start(bf16[2,4,32,2048]{3,2,1,0:T(8,128)(2,1)} %copy-done.8) | copy-start | bytes 3145732
  846.9 41.2 %all-to-all-start.4 = ((bf16[256,8,256]{2,1,0:T(8,128)(2,1)}), bf16[256,8,256]{2,1,0:T(8,128)(2,1)}, u32[]{:S(2)}, u32[]{:S(2)}) async-start(bf16[256,8,256]{2,1,0:T(8,128)(2,1)} %copy.142), calls=%async_computation.4 | async-start | bytes 2097152 | tf_op jit(solution)/shard_map/all_to_all | solution.py:25
  889.6 1.5 copy-start.3
  891.1 8.4 copy-start.10
Sparse Core Ops, SparseCore 0:
  9.9 733.4 all-gather.2
where the time goes:
time: 909 us; the launch traced here: 908 us
  waiting for transfers between devices  588 us (65%)
  blocking collectives  190 us (21%)
  starting transfers between devices  43.5 us (5%)
  local copies, waits for them, and re-layouts  35.9 us (4%)
  matrix products  30.1 us (3%)
  between operations  14.4 us (2%)
    all_gather x1, waiting for transfers between devices, body(): gathered = lax.all_gather(gate_weight, ALL, axis=0, tiled=True)  546 us
    all_gather x1, blocking collectives, body(): block_one = lax.all_gather(level_one[:, 0], 'sb', axis=0, tiled=True)  60.6 us
    all_to_all x1, blocking collectives, to_blocks(): parts = lax.all_to_all(parts, ALL, split_axis=0, concat_axis=0, tiled=True)  44.5 us
    all_to_all x1, blocking collectives, from_blocks(): parts = lax.all_to_all(parts, ALL, split_axis=0, concat_axis=0, tiled=True)  42.8 us
    all_gather x1, blocking collectives, body(): block_two = lax.all_gather(level_two, 'sb', axis=1, tiled=True)  42.1 us
    dot_general x11, matrix products, dot(): return jnp.einsum(pattern, left, right, preferred_element_type=jnp.float32)  30.1 us
    all_to_all x1, waiting for transfers between devices, from_blocks(): parts = lax.all_to_all(parts, ALL, split_axis=0, concat_axis=0, tiled=True)  24.2 us
  transfers between devices with their start and end apart: 6, of which 5 were waited for; matrix products, arithmetic and copies ran while one was open for 3% of the time, Pallas kernels for 0%

commit v1 on v0

--- a/solution.py
+++ b/solution.py
@@ -35,7 +35,9 @@
     channels = tokens.shape[3]
     sa, sb = (lax.axis_size("sa"), lax.axis_size("sb"))
     grad_scale = channels ** (-0.5)
-    gathered = lax.all_gather(gate_weight, ALL, axis=0, tiled=True)
+    gathered = jnp.concatenate(
+        lax.all_to_all(jnp.stack([gate_weight] * lax.axis_size(ALL)), ALL, 0, 0), axis=0
+    )
     block_one = lax.all_gather(level_one[:, 0], "sb", axis=0, tiled=True)
     block_two = lax.all_gather(level_two, "sb", axis=1, tiled=True)
     block_two = lax.all_to_all(block_two, "sa", split_axis=1, concat_axis=0, tiled=True)[:, 0]

time: 909 us -> 538 us (0.59)
  waiting for transfers between devices: 588 us -> 225 us
  between operations: 14.4 us -> 1.06 us
    all_gather x1 -> x0, waiting for transfers between devices: 546 us -> none  [body(): gathered = lax.all_gather(gate_weight, ALL, axis=0, tiled=True)]
    all_to_all x0 -> x1, waiting for transfers between devices: none -> 183 us  [body(): lax.all_to_all(jnp.stack([gate_weight] * lax.axis_size(ALL)), ALL, 0, 0)]
  transfers between devices with their start and end apart: 6 -> 6, of which waited for: 5 -> 5; matrix products, arithmetic and copies ran while one was open for 3% -> 4% of each run, Pallas kernels for 0% -> 0%
where the time goes in v1:
time: 538 us; the launch traced here: 537 us
  waiting for transfers between devices  225 us (42%)
  blocking collectives  183 us (34%)
  starting transfers between devices  52 us (10%)
  local copies, waits for them, and re-layouts  40.3 us (7%)
  matrix products  30.1 us (6%)
  other arithmetic  5.7 us (1%)
    all_to_all x1, waiting for transfers between devices, body(): lax.all_to_all(jnp.stack([gate_weight] * lax.axis_size(ALL)), ALL, 0, 0)  183 us
    all_gather x1, blocking collectives, body(): block_one = lax.all_gather(level_one[:, 0], 'sb', axis=0, tiled=True)  60.1 us
    all_to_all x1, blocking collectives, from_blocks(): parts = lax.all_to_all(parts, ALL, split_axis=0, concat_axis=0, tiled=True)  43.2 us
    all_gather x1, blocking collectives, body(): block_two = lax.all_gather(level_two, 'sb', axis=1, tiled=True)  41.9 us
    all_to_all x1, blocking collectives, to_blocks(): parts = lax.all_to_all(parts, ALL, split_axis=0, concat_axis=0, tiled=True)  37.4 us
    dot_general x11, matrix products, dot(): return jnp.einsum(pattern, left, right, preferred_element_type=jnp.float32)  30.1 us
    all_to_all x1, waiting for transfers between devices, from_blocks(): parts = lax.all_to_all(parts, ALL, split_axis=0, concat_axis=0, tiled=True)  24.2 us
    all_to_all x1, starting transfers between devices, body(): lax.all_to_all(block_two, 'sa', split_axis=1, concat_axis=0, tiled=True)  12.9 us
  transfers between devices with their start and end apart: 6, of which 5 were waited for; matrix products, arithmetic and copies ran while one was open for 4% of the time, Pallas kernels for 0%

profile of v1, /device:TPU:1, one launch (start us, length us, event | category | flops | bytes accessed | tf_op | source)
XLA Modules:
  0.0 536.7 jit_solution(1056388482337025485)
XLA Ops:
  0.7 0.9 copy.129
  1.6 41.9 %all_gather.7 = bf16[2,32,32,32]{3,2,0,1:T(8,128)(2,1)S(1)} all-gather(bf16[2,4,32,32]{3,2,0,1:T(8,128)(2,1)S(1)} %copy.129), channel_id=1, replica_groups=mesh['sa'=32,'sb'=8] {'sb'}, dimensions={1}, use_global_device_ids=true | all-gather | bytes 147456 | tf_op jit(solution)/shard_map/all_gather | solution.py:42
  43.5 1.2 reshape.147
  44.7 12.9 %all-to-all-start.1 = ((bf16[32,2,1024]{2,1,0:T(2,128)(2,1)}), bf16[32,2,1024]{2,1,0:T(2,128)(2,1)S(1)}, u32[]{:S(2)}, u32[]{:S(2)}) async-start(bf16[32,2,1024]{2,1,0:T(2,128)(2,1)} %reshape.147), calls=%async_computation.1 | async-start | bytes 262144 | tf_op jit(solution)/shard_map/all_to_all | solution.py:43
  57.6 0.3 fusion.16
  57.9 0.3 fusion.18
  58.2 0.3 copy.159
  58.6 1.6 copy.154
  60.1 6.0 %all-to-all-done.1 = bf16[32,2,1024]{2,1,0:T(2,128)(2,1)S(1)} async-done(((bf16[32,2,1024]{2,1,0:T(2,128)(2,1)}), bf16[32,2,1024]{2,1,0:T(2,128)(2,1)S(1)}, u32[]{:S(2)}, u32[]{:S(2)}) %all-to-all-start.1) | async-done | bytes 131104 | tf_op jit(solution)/shard_map/all_to_all | solution.py:43
  66.1 9.9 %all-to-all-start = ((bf16[256,8,256]{2,1,0:T(8,128)(2,1)}), bf16[256,8,256]{2,1,0:T(8,128)(2,1)S(1)}, u32[]{:S(2)}, u32[]{:S(2)}) async-start(bf16[256,8,256]{2,1,0:T(8,128)(2,1)} %copy.154), calls=%async_computation | async-start | bytes 2097152 | tf_op jit(solution)/shard_map/all_to_all | solution.py:15
  76.0 60.1 %all-gather = bf16[32,1,64,64]{3,2,1,0:T(8,128)(2,1)S(1)} all-gather(bf16[4,1,64,64]{3,2,1,0:T(8,128)(2,1)S(1)} %copy-done.12), channel_id=2, replica_groups=mesh['sa'=32,'sb'=8] {'sb'}, dimensions={0}, use_global_device_ids=true | all-gather | bytes 294912 | tf_op jit(solution)/shard_map/all_gather | solution.py:41
  136.2 0.3 reshape.148
  136.4 0.2 copy.127
  136.7 1.1 copy.128
  137.8 0.4 reshape.128
  138.2 0.4 fusion.25
  138.6 1.7 fusion.26
  140.4 1.3 reshape.129
  141.9 0.6 copy.132
  142.5 43.2 %all_to_all.64 = bf16[256,8,256]{2,1,0:T(8,128)(2,1)S(1)} all-to-all(bf16[256,8,256]{2,1,0:T(8,128)(2,1)S(1)} %copy.132), channel_id=1, replica_groups=mesh['sa'=32,'sb'=8] {'sa','sb'}, dimensions={0} | all-to-all | bytes 2097152 | tf_op jit(solution)/shard_map/all_to_all | solution.py:25
  185.7 4.3 stack.2
  190.0 8.4 %all-to-all-start.3 = ((bf16[256,8,2048]{2,1,0:T(8,128)(2,1)}), bf16[256,8,2048]{2,1,0:T(8,128)(2,1)}, u32[]{:S(2)}, u32[]{:S(2)}) async-start(bf16[256,8,2048]{2,1,0:T(8,128)(2,1)} %stack.2), calls=%async_computation.3 | async-start | bytes 16777216 | tf_op jit(solution)/shard_map/all_to_all | solution.py:39
  198.4 1.2 copy.155
  199.6 1.6 reshape.132
  201.2 1.8 convolution_bitcast_fusion
  202.9 183.2 %all-to-all-done.3 = bf16[256,8,2048]{2,1,0:T(8,128)(2,1)} async-done(((bf16[256,8,2048]{2,1,0:T(8,128)(2,1)}), bf16[256,8,2048]{2,1,0:T(8,128)(2,1)}, u32[]{:S(2)}, u32[]{:S(2)}) %all-to-all-start.3) | async-done | bytes 8388640 | tf_op jit(solution)/shard_map/all_to_all | solution.py:39
  386.1 9.3 %fusion.10 = (bf16[2,4,32,2048]{3,2,1,0:T(8,128)(2,1)S(1)}, bf16[2,4,32,2048]{3,2,1,0:T(8,128)(2,1)}, f32[2,4,32,2048]{3,2,1,0:T(8,128)}) fusion(bf16[2,4,32,2048]{3,2,1,0:T(8,128)(2,1)} %param.13, f32[2,4,32,2048]{3,2,1,0:T(8,128)} %convolution_bitcast_fusion, bf16[2,4,32,2048]{3,2,1,0:T(8,128)(2,1)} %param.7, bf16[256,8,2048]{2,1,0:T(8,128)(2,1)} %all-to-all-done.3, ...), kind=kOutput, calls=%fused_computation.16 | convolution fusion | flops 2155347968 | bytes 16786432 | tf_op jit(solution)/shard_map/tr,rc->tc/dot_general | solution.py:31
  395.5 0.5 convolution_convert_fusion
  395.9 0.3 copy.160
  396.4 0.6 copy.156
  397.0 37.4 %all_to_all.65 = bf16[256,8,256]{2,1,0:T(8,128)(2,1)S(1)} all-to-all(bf16[256,8,256]{2,1,0:T(8,128)(2,1)S(1)} %copy.156), channel_id=1, replica_groups=mesh['sa'=32,'sb'=8] {'sa','sb'}, dimensions={0} | all-to-all | bytes 2097152 | tf_op jit(solution)/shard_map/all_to_all | solution.py:15
  434.4 0.2 copy.136
  434.6 2.3 copy.137
  437.0 2.2 reshape.137
  439.1 2.9 fusion.27
  442.1 0.5 fusion.23
  442.5 2.2 reshape.149
  444.8 5.9 %all-to-all-start.6 = ((bf16[32,2,1024]{2,1,0:T(2,128)(2,1)}), bf16[32,2,1024]{2,1,0:T(2,128)(2,1)}, u32[]{:S(2)}, u32[]{:S(2)}) async-start(bf16[32,2,1024]{2,1,0:T(2,128)(2,1)} %reshape.149), calls=%async_computation.6 | async-start | bytes 262144 | tf_op jit(solution)/shard_map/all_to_all | solution.py:70
  450.7 1.5 convolution_convert_fusion.6
  452.2 1.5 reshape.140
  453.7 5.6 %all-to-all-done.6 = bf16[32,2,1024]{2,1,0:T(2,128)(2,1)} async-done(((bf16[32,2,1024]{2,1,0:T(2,128)(2,1)}), bf16[32,2,1024]{2,1,0:T(2,128)(2,1)}, u32[]{:S(2)}, u32[]{:S(2)}) %all-to-all-start.6) | async-done | bytes 131104 | tf_op jit(solution)/shard_map/all_to_all | solution.py:70
  459.3 1.2 reshape.150
  460.6 1.2 reshape.142
  461.8 0.9 maximum_bitcast_fusion
  462.8 0.5 broadcast.61
  463.3 1.6 reduce.1
  464.9 2.0 reshape.151
  466.9 4.1 all-to-all-start.7
  471.0 1.9 fusion.24
  472.9 1.5 reshape.138
  474.4 0.6 copy.141
  475.0 1.6 copy.142
  476.5 6.0 %all-to-all-done.7 = bf16[8,2,12288]{2,1,0:T(2,128)(2,1)} async-done(((bf16[8,2,12288]{2,1,0:T(2,128)(2,1)}), bf16[8,2,12288]{2,1,0:T(2,128)(2,1)}, u32[]{:S(2)}, u32[]{:S(2)}) %all-to-all-start.7) | async-done | bytes 393248 | tf_op jit(solution)/shard_map/all_to_all | solution.py:81
  482.5 10.8 %all-to-all-start.5 = ((bf16[256,8,256]{2,1,0:T(8,128)(2,1)}), bf16[256,8,256]{2,1,0:T(8,128)(2,1)}, u32[]{:S(2)}, u32[]{:S(2)}) async-start(bf16[256,8,256]{2,1,0:T(8,128)(2,1)} %copy.142), calls=%async_computation.5 | async-start | bytes 2097152 | tf_op jit(solution)/shard_map/all_to_all | solution.py:25
  493.3 1.1 convolution_multiply_fusion
  494.4 2.6 reshape.152
  497.0 1.0 convert_reduce_fusion
  498.0 0.7 slice.15
  498.8 0.7 slice.17
  499.5 24.2 %all-to-all-done.5 = bf16[256,8,256]{2,1,0:T(8,128)(2,1)} async-done(((bf16[256,8,256]{2,1,0:T(8,128)(2,1)}), bf16[256,8,256]{2,1,0:T(8,128)(2,1)}, u32[]{:S(2)}, u32[]{:S(2)}) %all-to-all-start.5) | async-done | bytes 1048608 | tf_op jit(solution)/shard_map/all_to_all | solution.py:25
  523.7 1.4 copy.157
  525.2 1.5 reshape.143
  526.7 8.4 %fusion.21 = (f32[2,4,32]{2,1,0:T(4,128)S(1)}, f32[2,4,32,2048]{3,2,1,0:T(8,128)S(1)}) fusion(bf16[2,4,32,2048]{3,2,1,0:T(8,128)(2,1)S(1)} %copy-done.4, f32[2048]{0:T(1024)S(1)} %copy-done.14, f32[2,4,32,2048]{3,2,1,0:T(8,128)} %reshape.143, bf16[256,8,2048]{2,1,0:T(8,128)(2,1)} %all-to-all-done.3, f32[2,4,32,2048]{3,2,1,0:T(8,128)} %convolution_bitcast_fusion, ...), kind=kOutput, calls=%fused_computation.27 | convolution fusion | flops 2155872000 | bytes 18883584 | tf_op jit(solution)/shard_map/tc,rc->tr/dot_general | solution.py:31
  535.1 1.6 fusion.15
  (38 shorter events, 0.5 us)
Async XLA Ops:
  0.6 200.5 %copy-start = (bf16[2,4,32,32]{3,2,1,0:T(8,128)(2,1)S(1)}, bf16[2,4,32,32]{3,2,1,0:T(8,128)(2,1)}, u32[]{:S(2)}) copy-start(bf16[2,4,32,32]{3,2,1,0:T(8,128)(2,1)} %param.12) | copy-start | bytes 49156
  0.6 57.0 %copy-start.3 = (bf16[2,4,32,2048]{3,2,1,0:T(8,128)(2,1)S(1)}, bf16[2,4,32,2048]{3,2,1,0:T(8,128)(2,1)}, u32[]{:S(2)}) copy-start(bf16[2,4,32,2048]{3,2,1,0:T(8,128)(2,1)} %param.7) | copy-start | bytes 3145732
  0.7 57.3 %copy-start.14 = (f32[2048]{0:T(1024)S(1)}, f32[2048]{0:T(1024)}, u32[]{:S(2)}) copy-start(f32[2048]{0:T(1024)} %param.8) | copy-start | bytes 24580
  44.7 21.4 %all-to-all-start.1 = ((bf16[32,2,1024]{2,1,0:T(2,128)(2,1)}), bf16[32,2,1024]{2,1,0:T(2,128)(2,1)S(1)}, u32[]{:S(2)}, u32[]{:S(2)}) async-start(bf16[32,2,1024]{2,1,0:T(2,128)(2,1)} %reshape.147), calls=%async_computation.1 | async-start | bytes 262144 | tf_op jit(solution)/shard_map/all_to_all | solution.py:43
  58.5 17.5 %copy-start.12 = (bf16[4,1,64,64]{3,2,1,0:T(8,128)(2,1)S(1)}, bf16[4,1,64,64]{3,2,1,0:T(8,128)(2,1)}, u32[]{:S(2)}) copy-start(bf16[4,1,64,64]{3,2,1,0:T(8,128)(2,1)} %param.10) | copy-start | bytes 98308
  66.1 70.3 %all-to-all-start = ((bf16[256,8,256]{2,1,0:T(8,128)(2,1)}), bf16[256,8,256]{2,1,0:T(8,128)(2,1)S(1)}, u32[]{:S(2)}, u32[]{:S(2)}) async-start(bf16[256,8,256]{2,1,0:T(8,128)(2,1)} %copy.154), calls=%async_computation | async-start | bytes 2097152 | tf_op jit(solution)/shard_map/all_to_all | solution.py:15
  136.2 2.0 copy-start.7
  136.4 2.2 copy-start.5
  141.9 43.8 %copy-start.13 = (bf16[8,2048]{1,0:T(8,128)(2,1)S(1)}, bf16[8,2048]{1,0:T(8,128)(2,1)}, u32[]{:S(2)}) copy-start(bf16[8,2048]{1,0:T(8,128)(2,1)} %param.9) | copy-start | bytes 98308
  190.0 196.1 %all-to-all-start.3 = ((bf16[256,8,2048]{2,1,0:T(8,128)(2,1)}), bf16[256,8,2048]{2,1,0:T(8,128)(2,1)}, u32[]{:S(2)}, u32[]{:S(2)}) async-start(bf16[256,8,2048]{2,1,0:T(8,128)(2,1)} %stack.2), calls=%async_computation.3 | async-start | bytes 16777216 | tf_op jit(solution)/shard_map/all_to_all | solution.py:39
  395.4 1.0 copy-start.9
  439.1 2.9 copy-start.2
  439.1 2.9 copy-start.6
  444.8 14.5 %all-to-all-start.6 = ((bf16[32,2,1024]{2,1,0:T(2,128)(2,1)}), bf16[32,2,1024]{2,1,0:T(2,128)(2,1)}, u32[]{:S(2)}, u32[]{:S(2)}) async-start(bf16[32,2,1024]{2,1,0:T(2,128)(2,1)} %reshape.149), calls=%async_computation.6 | async-start | bytes 262144 | tf_op jit(solution)/shard_map/all_to_all | solution.py:70
  460.6 10.4 %copy-start.8 = (bf16[32,1,64,64]{3,2,1,0:T(8,128)(2,1)S(1)}, bf16[32,1,64,64]{3,2,1,0:T(8,128)(2,1)}, u32[]{:S(2)}) copy-start(bf16[32,1,64,64]{3,2,1,0:T(8,128)(2,1)} %copy-done.7) | copy-start | bytes 786436
  466.9 15.6 %all-to-all-start.7 = ((bf16[8,2,12288]{2,1,0:T(2,128)(2,1)}), bf16[8,2,12288]{2,1,0:T(2,128)(2,1)}, u32[]{:S(2)}, u32[]{:S(2)}) async-start(bf16[8,2,12288]{2,1,0:T(2,128)(2,1)} %reshape.151), calls=%async_computation.7 | async-start | bytes 786432 | tf_op jit(solution)/shard_map/all_to_all | solution.py:81
  475.0 18.3 %copy-start.10 = (bf16[2,4,32,2048]{3,2,1,0:T(8,128)(2,1)S(1)}, bf16[2,4,32,2048]{3,2,1,0:T(8,128)(2,1)}, u32[]{:S(2)}) copy-start(bf16[2,4,32,2048]{3,2,1,0:T(8,128)(2,1)} %copy-done.9) | copy-start | bytes 3145732
  482.5 41.2 %all-to-all-start.5 = ((bf16[256,8,256]{2,1,0:T(8,128)(2,1)}), bf16[256,8,256]{2,1,0:T(8,128)(2,1)}, u32[]{:S(2)}, u32[]{:S(2)}) async-start(bf16[256,8,256]{2,1,0:T(8,128)(2,1)} %copy.142), calls=%async_computation.5 | async-start | bytes 2097152 | tf_op jit(solution)/shard_map/all_to_all | solution.py:25
  525.1 1.5 copy-start.4
  526.7 8.5 %copy-start.11 = (bf16[2,4,32,2048]{3,2,1,0:T(8,128)(2,1)S(1)}, bf16[2,4,32,2048]{3,2,1,0:T(8,128)(2,1)}, u32[]{:S(2)}) copy-start(bf16[2,4,32,2048]{3,2,1,0:T(8,128)(2,1)} %param.13) | copy-start | bytes 3145732
  535.1 1.6 copy-start.1
